TPU v7x, 32 devices: a whole 2x2x4 slice. The times are simulated.
32 devices in a mesh: gz: 16 (over z, y, x), ta: 2 (over core).
Axes of the slice: x: 2, y: 2, z: 4, core: 2. Of those that a mesh axis runs over, the one named last changes fastest.
Arguments:
- position: float32 [2, 48, 32, 512], P(None, 'gz', 'ta'), may hold values from -6 to 6
- gaps: float32 [2, 3, 48, 32, 512], P(None, None, 'gz', 'ta'), may hold values from -6 to 6
- weights: float32 [3, 48, 32, 512], P(None, 'gz', 'ta'), may hold values from 0.2 to 2
- deltas: int32 [3, 48, 32, 512], P(None, 'gz', 'ta'), may hold values from 0 to 8
- springs: int32 [2, 48, 32, 512], P(None, 'gz', 'ta'), may hold values 0 or 1
- damping: float32 [48, 32, 512], P('gz', 'ta'), may hold values from 0.1 to 1
- stiffness: float32 [2, 48], P(None, 'gz'), may hold values from 0.5 to 4
Outputs:
- update: float32 [2, 48, 32, 512], P(None, 'gz', 'ta')
- residual: float32 [2, 48, 32, 512], P(None, 'gz', 'ta')
All inputs are finite; a program needn't handle non-finite values. No bound on the sum of `springs` on one device may be relied on, other than what follows from the above.
Results may differ from a plain program's by a relative error of at most 0.00012.
Values sent between devices are 32-bit elements; how exact they have to be, the bound alone decides.
A program may use at most 64 MiB of HBM per device.

v0:
```python
import functools

import jax
import jax.numpy as jnp
from jax import lax
from jax.experimental import pallas as pl
from jax.experimental.pallas import tpu as pltpu
from jax.sharding import PartitionSpec as P

MESH = pl.DeviceIdType.MESH
PLACES = 9
HALF = 8
OPS = 3


def rolled(values, step):
    axis = values.ndim - 1
    return values if step == 0 else pltpu.roll(values, step % values.shape[axis], axis)


def kernel(
    n, pos_h, gaps_h, wei_h, del_h, spr_h, dam_h, stiff,
    upd, res,
    v, up, tsend, trecv, esend, erecv, sall, gath,
    gaps, wei, dlt, spr, dam, vc, hc, hl, diag, qbuf,
    load_sem, vs_sem, vr_sem, ts_sem, tr_sem, es_sem, er_sem, gs_sem, gr_sem,
):
    g = lax.axis_index("gz")
    t = lax.axis_index("ta")
    secs, rows, cols = dam_h.shape
    chunks = rows // HALF
    other = {"gz": g, "ta": 1 - t}
    lower = {"gz": g - 1, "ta": t}
    upper = {"gz": g + 1, "ta": t}
    has_lower = g > 0
    has_upper = g < n - 1
    base = HALF

    loads = [
        pltpu.make_async_copy(pos_h, v.at[0, :, :, pl.ds(base, rows)], load_sem.at[0]),
        pltpu.make_async_copy(del_h, dlt, load_sem.at[1]),
        pltpu.make_async_copy(wei_h, wei, load_sem.at[2]),
        pltpu.make_async_copy(gaps_h, gaps, load_sem.at[3]),
        pltpu.make_async_copy(spr_h, spr, load_sem.at[4]),
        pltpu.make_async_copy(dam_h, dam, load_sem.at[5]),
    ]
    for load in loads:
        load.start()

    barrier = pltpu.get_barrier_semaphore()
    pl.semaphore_signal(barrier, inc=1, device_id=other, device_id_type=MESH)
    for j in range(1, n):
        pl.semaphore_signal(
            barrier, inc=1, device_id={"gz": lax.rem(g + j, n), "ta": t}, device_id_type=MESH
        )

    @pl.when(jnp.logical_not(has_upper))
    def _():
        up[...] = jnp.zeros_like(up)

    @pl.when(jnp.logical_not(has_lower))
    def _():
        trecv[...] = jnp.zeros_like(trecv)

    esend[...] = jnp.zeros_like(esend)

    def rows_at(h):
        return pl.ds(h * HALF, HALF)

    def v_copy(op, h):
        return pltpu.make_async_remote_copy(
            v.at[op, :, :, pl.ds(base + h * HALF, HALF)], up.at[op, :, :, rows_at(h)],
            vs_sem.at[op, h], vr_sem.at[op, h], device_id=lower, device_id_type=MESH,
        )

    def comps(op):
        return 3 if op == 0 else 2

    def t_copy(op, h):
        part = pl.ds(0, comps(op))
        return pltpu.make_async_remote_copy(
            tsend.at[op, part, :, rows_at(h)], trecv.at[op, part, :, rows_at(h)],
            ts_sem.at[op, h], tr_sem.at[op, h], device_id=upper, device_id_type=MESH,
        )

    def e_copy(op):
        return pltpu.make_async_remote_copy(
            esend.at[op], erecv.at[op], es_sem.at[op], er_sem.at[op],
            device_id=other, device_id_type=MESH,
        )

    def send_edges(op):
        for comp in range(2):
            for z in range(secs):
                top = v[op, comp, z, base : base + 1, :]
                bottom = v[op, comp, z, base + rows - 1 : base + rows, :]
                k = comp * secs + z
                esend[op, k : k + 1, :] = jnp.where(t == 0, bottom, top)
        if op == 0:
            for z in range(secs):
                k = 2 * secs + z
                esend[op, k : k + 1, :] = jnp.where(
                    spr[1, z, rows - 1 : rows, :] > 0, 1.0, 0.0
                ).astype(jnp.float32)
        e_copy(op).start()

    def take_edges(op):
        e_copy(op).wait_recv()
        for comp in range(2):
            for z in range(secs):
                k = comp * secs + z
                row = erecv[op, k : k + 1, :]
                v[op, comp, z, base - 1 : base, :] = jnp.where(t == 1, row, 0.0)
                v[op, comp, z, base + rows : base + rows + 1, :] = jnp.where(t == 0, row, 0.0)
        if op == 0:
            for z in range(secs):
                k = 2 * secs + z
                row = stiff[1, z] * erecv[op, k : k + 1, :]
                vc[z, base - 1 : base, :] = jnp.where(t == 1, row, 0.0)

    def scatter(op, h, dest):
        sources = [(dest - k - 1, k) for k in range(3) if 0 <= dest - k - 1 < secs]
        terms = []
        for z, k in sources:
            w = wei[k, z, rows_at(h)]
            field = v[op, :, z, pl.ds(base + h * HALF, HALF)]
            if op == 0:
                field = field - gaps[:, k, z, rows_at(h)]
                u = jnp.concatenate([w[None] * field, w[None]], 0)
            else:
                u = w[None] * field
            terms.append((dlt[k, z, rows_at(h)], u))
        total = None
        for place in range(PLACES):
            part = None
            for d, u in terms:
                one = jnp.where((d == place)[None], u, 0.0)
                part = one if part is None else part + one
            part = rolled(part, place - 4)
            total = part if total is None else total + part
        return total

    def send_up(op, h):
        for d in range(secs):
            tsend[op, pl.ds(0, comps(op)), d, rows_at(h)] = scatter(op, h, secs + d)

        @pl.when(has_upper)
        def _():
            t_copy(op, h).start()

    def send_down(op, h):
        @pl.when(has_lower)
        def _():
            v_copy(op, h).start()

    loads[0].wait()
    pl.semaphore_wait(barrier, n)
    send_down(0, 0)

    loads[1].wait()
    loads[2].wait()
    shape = (HALF, cols)
    columns_at = lax.broadcasted_iota(jnp.int32, shape, 1)
    row_at = lax.broadcasted_iota(jnp.int32, shape, 0)
    for k in range(3):
        for z in range(secs):
            inside = jnp.where(g * secs + z + k + 1 < n * secs, 1.0, 0.0).astype(jnp.float32)
            for h in range(chunks):
                target = columns_at + dlt[k, z, rows_at(h)] - 4
                valid = (target >= 0) & (target < cols)
                wei[k, z, rows_at(h)] = jnp.where(valid, wei[k, z, rows_at(h)], 0.0) * inside
    loads[3].wait()
    for h in range(chunks):
        send_up(0, h)
        if h + 1 < chunks:
            send_down(0, h + 1)
    loads[4].wait()
    send_edges(0)
    loads[5].wait()
    vc[...] = jnp.zeros_like(vc)
    for z in range(secs):
        for h in range(chunks):
            last = jnp.where((t == 1) & (row_at == HALF - 1), 0.0, 1.0) if h == chunks - 1 else 1.0
            vc[z, pl.ds(base + h * HALF, HALF)] = (
                stiff[1, z] * jnp.where(spr[1, z, rows_at(h)] > 0, 1.0, 0.0).astype(jnp.float32) * last
            )
            right = stiff[0, z] * jnp.where(
                (spr[0, z, rows_at(h)] > 0) & (columns_at < cols - 1), 1.0, 0.0
            ).astype(jnp.float32)
            hc[z, rows_at(h)] = right
            left = rolled(right, 1)
            hl[z, rows_at(h)] = left
            total = dam[z, rows_at(h)] + right + left
            for k in range(3):
                total = total + wei[k, z, rows_at(h)]
            diag[z, rows_at(h)] = total

    def local(op, h, write):
        here = pl.ds(base + h * HALF, HALF)
        own = {}
        for d in range(1, secs):
            own[d] = scatter(op, h, d)
            if op == 0:
                diag[d, rows_at(h)] = diag[d, rows_at(h)] + own[d][2]
        acc = [None] * secs
        for z in range(secs):
            center = v[op, :, z, here]
            acc[z] = -(
                hc[z, rows_at(h)][None] * rolled(center, -1)
                + hl[z, rows_at(h)][None] * rolled(center, 1)
            )
            if z > 0:
                acc[z] = acc[z] - own[z][0:2]
            if op == 0:
                for k in range(3):
                    acc[z] = acc[z] - wei[k, z, rows_at(h)][None] * gaps[:, k, z, rows_at(h)]

        def gather(s):
            field = v[op, :, s, here] if s < secs else up[op, :, s - secs, rows_at(h)]
            sources = [(s - k - 1, k) for k in range(3) if 0 <= s - k - 1 < secs]
            got = [None] * len(sources)
            for place in range(PLACES):
                moved = rolled(field, 4 - place)
                for i, (z, k) in enumerate(sources):
                    if got[i] is None:
                        got[i] = moved
                    else:
                        got[i] = jnp.where((dlt[k, z, rows_at(h)] == place)[None], moved, got[i])
            for i, (z, k) in enumerate(sources):
                acc[z] = acc[z] - wei[k, z, rows_at(h)][None] * got[i]

        for s in range(1, secs):
            gather(s)
        if h == 0:
            take_edges(op)
        for z in range(secs):
            if op == 0:
                above = vc[z, base + h * HALF - 1 : base + h * HALF - 1 + HALF, :]
                diag[z, rows_at(h)] = diag[z, rows_at(h)] + vc[z, here] + above
            first = base + h * HALF
            acc[z] = acc[z] - (
                vc[z, here][None] * v[op, :, z, first + 1 : first + 1 + HALF, :]
                + vc[z, first - 1 : first - 1 + HALF, :][None]
                * v[op, :, z, first - 1 : first - 1 + HALF, :]
            )

        @pl.when(has_lower)
        def _():
            t_copy(op, h).wait_recv()

        @pl.when(has_upper)
        def _():
            v_copy(op, h).wait_recv()

        for s in range(secs, 2 * secs):
            gather(s)
        for z in range(secs):
            if op == 0:
                diag[z, rows_at(h)] = diag[z, rows_at(h)] + trecv[op, 2, z, rows_at(h)]
            image = (
                acc[z]
                + diag[z, rows_at(h)][None] * v[op, :, z, here]
                - trecv[op, 0:2, z, rows_at(h)]
            )
            write(z, image)

    dots = [jnp.zeros(shape, jnp.float32) for _ in range(4)]

    def dot_into(i, a, b):
        dots[i] = dots[i] + a[0] * b[0] + a[1] * b[1]

    for op in range(OPS):
        for h in range(chunks):
            here = pl.ds(base + h * HALF, HALF)

            def write(z, image, op=op, h=h, here=here):
                if op == 0:
                    v[1, :, z, here] = -image
                    dot_into(0, image, image)
                elif op == 1:
                    v[2, :, z, here] = image
                    dot_into(1, v[1, :, z, here], image)
                    dot_into(2, image, image)
                else:
                    qbuf[:, z, rows_at(h)] = image
                    dot_into(3, v[2, :, z, here], image)

            local(op, h, write)
            if op + 1 < OPS:
                send_down(op + 1, h)
                send_up(op + 1, h)
        if op + 1 < OPS:
            send_edges(op + 1)

    lanes = 128
    packed = jnp.zeros((8, lanes), jnp.float32)
    sub = lax.broadcasted_iota(jnp.int32, (8, lanes), 0)
    for i in range(4):
        row = jnp.sum(dots[i], axis=0, keepdims=True)
        part = row[:, 0:lanes]
        for c in range(lanes, cols, lanes):
            part = part + row[:, c : c + lanes]
        packed = jnp.where(sub == i, part, packed)
    esend[OPS, 0:8, 0:lanes] = packed
    e_copy(OPS).start()
    e_copy(OPS).wait_recv()
    packed = packed + erecv[OPS, 0:8, 0:lanes]
    sall[...] = packed
    pushes = []
    for j in range(1, n):
        pushes.append(
            pltpu.make_async_remote_copy(
                sall, gath.at[j - 1], gs_sem.at[j - 1], gr_sem.at[j - 1],
                device_id={"gz": lax.rem(g + j, n), "ta": t}, device_id_type=MESH,
            )
        )
    for push in pushes:
        push.start()
    for push in pushes:
        push.wait_recv()
    total = packed
    for j in range(1, n):
        total = total + gath[j - 1]
    total = jnp.sum(total, axis=1, keepdims=True)
    rr, rm, mm, mq = (total[i : i + 1, :] for i in range(4))
    alpha0 = rr / rm
    rr1 = alpha0 * (alpha0 * mm) - rr
    ratio = rr1 / rr
    one = 1.0 + ratio
    curve = one * one * rm - 2.0 * one * alpha0 * mm + alpha0 * alpha0 * mq
    alpha1 = rr1 / curve
    for z in range(secs):
        for h in range(chunks):
            here = pl.ds(base + h * HALF, HALF)
            for comp in range(2):
                r0 = v[1, comp, z, here]
                m0 = v[2, comp, z, here]
                q = qbuf[comp, z, rows_at(h)]
                r1 = r0 - alpha0 * m0
                upd[comp, z, rows_at(h)] = alpha0 * r0 + alpha1 * (r1 + ratio * r0)
                res[comp, z, rows_at(h)] = r1 - alpha1 * (one * m0 - alpha0 * q)

    for push in pushes:
        push.wait_send()
    for op in range(OPS + 1):
        e_copy(op).wait_send()

    @pl.when(has_lower)
    def _():
        for op in range(OPS):
            for h in range(chunks):
                v_copy(op, h).wait_send()

    @pl.when(has_upper)
    def _():
        for op in range(OPS):
            for h in range(chunks):
                t_copy(op, h).wait_send()


def body(position, gaps, weights, deltas, springs, damping, stiffness):
    secs, rows, cols = damping.shape
    n = lax.axis_size("gz")
    chunks = rows // HALF
    f32, i32 = jnp.float32, jnp.int32
    edge = -(-3 * secs // 8) * 8
    padded = rows + 2 * HALF
    dma = pltpu.SemaphoreType.DMA
    out = jax.ShapeDtypeStruct(position.shape, f32)
    anyspace = pl.BlockSpec(memory_space=pl.ANY)
    vmem = pl.BlockSpec(memory_space=pltpu.VMEM)
    return pl.pallas_call(
        functools.partial(kernel, n),
        out_shape=(out, out),
        in_specs=[anyspace] * 6 + [pl.BlockSpec(memory_space=pltpu.SMEM)],
        out_specs=(vmem, vmem),
        scratch_shapes=[
            pltpu.VMEM((OPS, 2, secs, padded, cols), f32),
            pltpu.VMEM((OPS, 2, secs, rows, cols), f32),
            pltpu.VMEM((OPS, 3, secs, rows, cols), f32),
            pltpu.VMEM((OPS, 3, secs, rows, cols), f32),
            pltpu.VMEM((OPS + 1, edge, cols), f32),
            pltpu.VMEM((OPS + 1, edge, cols), f32),
            pltpu.VMEM((8, 128), f32),
            pltpu.VMEM((n - 1, 8, 128), f32),
            pltpu.VMEM(gaps.shape, f32),
            pltpu.VMEM(weights.shape, f32),
            pltpu.VMEM(deltas.shape, i32),
            pltpu.VMEM(springs.shape, i32),
            pltpu.VMEM(damping.shape, f32),
            pltpu.VMEM((secs, padded, cols), f32),
            pltpu.VMEM(damping.shape, f32),
            pltpu.VMEM(damping.shape, f32),
            pltpu.VMEM(damping.shape, f32),
            pltpu.VMEM(position.shape, f32),
            dma((6,)),
            dma((OPS, chunks)), dma((OPS, chunks)),
            dma((OPS, chunks)), dma((OPS, chunks)),
            dma((OPS + 1,)), dma((OPS + 1,)),
            dma((n - 1,)), dma((n - 1,)),
        ],
        compiler_params=pltpu.CompilerParams(
            collective_id=0, has_side_effects=True, vmem_limit_bytes=67043328
        ),
    )(position, gaps, weights, deltas, springs, damping, stiffness)


def solution(mesh):
    return jax.shard_map(
        body,
        mesh=mesh,
        in_specs=(
            P(None, "gz", "ta", None),
            P(None, None, "gz", "ta", None),
            P(None, "gz", "ta", None),
            P(None, "gz", "ta", None),
            P(None, "gz", "ta", None),
            P("gz", "ta", None),
            P(None, "gz"),
        ),
        out_specs=(P(None, "gz", "ta", None), P(None, "gz", "ta", None)),
        check_vma=False,
    )
```

profile of v0, /device:TPU:0, one launch (start us, length us, event | category | flops | bytes accessed | tf_op | source)
XLA Modules:
  0.0 47.9 jit_solution(3278341376162970591)
XLA Ops:
  0.6 44.9 %shard_map.86 = (f32[2,3,16,512]{3,2,1,0:T(8,128)}, f32[2,3,16,512]{3,2,1,0:T(8,128)}) custom-call(f32[2,3,16,512]{3,2,1,0:T(8,128)} %pos_h.1, f32[2,3,3,16,512]{4,3,2,1,0:T(8,128)} %gaps_h.1, f32[3,3,16,512]{3,2,1,0:T(8,128)} %wei_h.1, s32[3,3,16,512]{3,2,1,0:T(8,128)} %del_h.1, s32[2,3,16,512]{3,2,1,0:T(8,128)} %spr_h.1, f32[3,16,512]{2,1,0:T(8,128)} %dam_h.1, ...), custom_call_target="tpu_custom_call" | custom-call | tf_op jit(solution)/shard_map/pallas_call | solution.py:372
  45.6 0.0 copy-start
  45.6 1.7 %copy.11 = f32[2,3,16,512]{3,2,1,0:T(8,128)} copy(f32[2,3,16,512]{3,2,1,0:T(8,128)} %get-tuple-element.4) | data formatting | bytes 393216
  47.2 0.0 copy-done
  47.3 0.7 %copy.12 = f32[2,3,16,512]{3,2,1,0:T(8,128)} copy(f32[2,3,16,512]{3,2,1,0:T(8,128)S(1)} %copy-done) | data formatting | bytes 393216
Async XLA Ops:
  45.6 1.7 %copy-start = (f32[2,3,16,512]{3,2,1,0:T(8,128)S(1)}, f32[2,3,16,512]{3,2,1,0:T(8,128)}, u32[]{:S(2)}) copy-start(f32[2,3,16,512]{3,2,1,0:T(8,128)} %get-tuple-element.5) | copy-start | bytes 589828
where the time goes:
time: 48.1 us; the launch traced here: 47.9 us
  Pallas kernels  44.9 us (93%)
  local copies, waits for them, and re-layouts  2.34 us (5%)
  between operations  0.65 us (1%)
    pallas_call x1, Pallas kernels, body(): pl.pallas_call(functools.partial(kernel, n), out_shape=(out, out), in_spe...  44.9 us
    unnamed x4, local copies, waits for them, and re-layouts  2.34 us

commit v1 on v0

v1 whole, which is shorter than its diff:
```python
import functools

import jax
import jax.numpy as jnp
from jax import lax
from jax.experimental import pallas as pl
from jax.experimental.pallas import tpu as pltpu
from jax.sharding import PartitionSpec as P

MESH = pl.DeviceIdType.MESH
PLACES = 9
HALF = 8
OPS = 3
LANES = 128
VMEM = 67043328


def rolled(values, step):
    axis = values.ndim - 1
    return values if step == 0 else pltpu.roll(values, step % values.shape[axis], axis)


def doublings(n):
    reach, out = 1, []
    while reach < n:
        out.append(reach)
        reach *= 2
    return out


def kernel(
    n, pos_h, gaps_h, wei_h, del_h, spr_h, dam_h, stiff,
    upd, res,
    pos, r0, m0, up, tsend, trecv, esend, erecv, sall, gath,
    gaps, wei, dlt, spr, dam, vc, va, hc, hl, diag, accb, qbuf, dots,
    load_sem, vs_sem, vr_sem, ts_sem, tr_sem, es_sem, er_sem, gs_sem, gr_sem, reach_sem,
):
    g = lax.axis_index("gz")
    t = lax.axis_index("ta")
    secs, rows, cols = dam_h.shape
    chunks = rows // HALF
    other = {"gz": g, "ta": 1 - t}
    lower = {"gz": g - 1, "ta": t}
    upper = {"gz": g + 1, "ta": t}
    has_lower = g > 0
    has_upper = g < n - 1
    fields = [pos, r0, m0]

    loads = [
        pltpu.make_async_copy(pos_h, pos, load_sem.at[0]),
        pltpu.make_async_copy(spr_h, spr, load_sem.at[1]),
        pltpu.make_async_copy(del_h, dlt, load_sem.at[2]),
        pltpu.make_async_copy(wei_h, wei, load_sem.at[3]),
        pltpu.make_async_copy(dam_h, dam, load_sem.at[4]),
        pltpu.make_async_copy(gaps_h, gaps, load_sem.at[5]),
    ]
    for load in loads:
        load.start()

    barrier = pltpu.get_barrier_semaphore()
    pl.semaphore_signal(barrier, inc=1, device_id=other, device_id_type=MESH)

    @pl.when(has_lower)
    def _():
        pl.semaphore_signal(barrier, inc=1, device_id=lower, device_id_type=MESH)

    @pl.when(has_upper)
    def _():
        pl.semaphore_signal(barrier, inc=1, device_id=upper, device_id_type=MESH)

    @pl.when(jnp.logical_not(has_upper))
    def _():
        up[...] = jnp.zeros_like(up)

    @pl.when(jnp.logical_not(has_lower))
    def _():
        trecv[...] = jnp.zeros_like(trecv)

    esend[...] = jnp.zeros_like(esend)
    dots[...] = jnp.zeros_like(dots)

    def rows_at(h):
        return pl.ds(h * HALF, HALF)

    def v_copy(op, d, h):
        return pltpu.make_async_remote_copy(
            fields[op].at[:, d, rows_at(h)], up.at[op, :, d, rows_at(h)],
            vs_sem.at[op, d * chunks + h], vr_sem.at[op, d * chunks + h], device_id=lower, device_id_type=MESH,
        )

    def t_copy(op, d, h):
        return pltpu.make_async_remote_copy(
            tsend.at[op, :, d, rows_at(h)], trecv.at[op, :, d, rows_at(h)],
            ts_sem.at[op, d * chunks + h], tr_sem.at[op, d * chunks + h], device_id=upper, device_id_type=MESH,
        )

    def e_copy(op):
        return pltpu.make_async_remote_copy(
            esend.at[op], erecv.at[op], es_sem.at[op], er_sem.at[op],
            device_id=other, device_id_type=MESH,
        )

    far = doublings(n)

    def reach_signal(i):
        for sign in (-1, 1):
            there = g + sign * far[i]

            @pl.when((there >= 0) & (there < n))
            def _():
                pl.semaphore_signal(
                    reach_sem.at[i], inc=1, device_id={"gz": there, "ta": t}, device_id_type=MESH
                )

    def reach_wait(i):
        pl.semaphore_wait(
            reach_sem.at[i],
            (g >= far[i]).astype(jnp.int32) + (g + far[i] < n).astype(jnp.int32),
        )

    pending = list(range(len(far)))

    def reach_step():
        if pending:
            i = pending.pop(0)
            reach_wait(i)
            if i + 1 < len(far):
                reach_signal(i + 1)

    def send_edges(op):
        for comp in range(2):
            for z in range(secs):
                k = comp * secs + z
                top = fields[op][comp, z, 0:1, :]
                bottom = fields[op][comp, z, rows - 1 : rows, :]
                esend[op, k : k + 1, :] = jnp.where(t == 0, bottom, top)
        if op == 0:
            for z in range(secs):
                k = 2 * secs + z
                esend[op, k : k + 1, :] = jnp.where(
                    spr[1, z, rows - 1 : rows, :] > 0, 1.0, 0.0
                ).astype(jnp.float32)
        e_copy(op).start()

    shape = (HALF, cols)
    columns_at = lax.broadcasted_iota(jnp.int32, shape, 1)
    row_at = lax.broadcasted_iota(jnp.int32, shape, 0)

    def dot_into(i, a, b):
        dots[i] = dots[i] + (a[0] * b[0] + a[1] * b[1])

    def pulls(op, s, h):
        field = fields[op][:, s, rows_at(h)] if s < secs else up[op, :, s - secs, rows_at(h)]
        sources = [(s - k - 1, k) for k in range(3) if 0 <= s - k - 1 < secs]
        got = [None] * len(sources)
        for place in range(PLACES):
            moved = rolled(field, 4 - place)
            for i, (z, k) in enumerate(sources):
                if got[i] is None:
                    got[i] = moved
                else:
                    got[i] = jnp.where((dlt[k, z, rows_at(h)] == place)[None], moved, got[i])
        out = []
        for i, (z, k) in enumerate(sources):
            miss = fields[op][:, z, rows_at(h)] - got[i]
            if op == 0:
                miss = miss - gaps[:, k, z, rows_at(h)]
            out.append((z, k, miss, wei[k, z, rows_at(h)][None] * miss))
        return out

    def scatter(terms, h):
        total = None
        for place in range(PLACES):
            part = None
            for z, k, _, pulled in terms:
                one = jnp.where((dlt[k, z, rows_at(h)] == place)[None], pulled, 0.0)
                part = one if part is None else part + one
            part = rolled(part, place - 4)
            total = part if total is None else total + part
        return total

    def own(op, h):
        here = rows_at(h)
        acc = []
        for z in range(secs):
            center = fields[op][:, z, here]
            acc.append(
                diag[z, here][None] * center
                - hc[z, here][None] * rolled(center, -1)
                - hl[z, here][None] * rolled(center, 1)
            )
        for s in range(1, secs):
            terms = pulls(op, s, h)
            for z, _, _, pulled in terms:
                acc[z] = acc[z] + pulled
            acc[s] = acc[s] - scatter(terms, h)
        for z in range(secs):
            accb[:, z, here] = acc[z]

    def vertical(op):
        for h in range(chunks):
            here = rows_at(h)
            for z in range(secs):
                for comp in range(2):
                    k = comp * secs + z
                    center = fields[op][comp, z, here]
                    if h == 0:
                        above = jnp.where(row_at == 0, erecv[op, k : k + 1, :], pltpu.roll(center, 1, 0))
                    else:
                        above = fields[op][comp, z, pl.ds(h * HALF - 1, HALF)]
                    if h == chunks - 1:
                        below = jnp.where(
                            row_at == HALF - 1, erecv[op, k : k + 1, :], pltpu.roll(center, HALF - 1, 0)
                        )
                    else:
                        below = fields[op][comp, z, pl.ds(h * HALF + 1, HALF)]
                    accb[comp, z, here] = accb[comp, z, here] - vc[z, here] * below - va[z, here] * above
                if op == OPS - 1:
                    dot_into(3, fields[op][:, z, here], accb[:, z, here])

    def cross(op, d, h):
        @pl.when(has_upper)
        def _():
            v_copy(op, d, h).wait_recv()

        terms = pulls(op, secs + d, h)
        tsend[op, :, d, rows_at(h)] = scatter(terms, h)

        @pl.when(has_upper)
        def _():
            t_copy(op, d, h).start()

        for z, _, miss, pulled in terms:
            accb[:, z, rows_at(h)] = accb[:, z, rows_at(h)] + pulled
            if op == OPS - 1:
                dot_into(3, miss, pulled)

    def finish(op, z, h):
        here = rows_at(h)

        @pl.when(has_lower)
        def _():
            t_copy(op, z, h).wait_recv()

        image = accb[:, z, here] - trecv[op, :, z, here]
        if op == 0:
            r0[:, z, here] = -image
        elif op == 1:
            m0[:, z, here] = image
        else:
            qbuf[:, z, here] = image
        if op + 1 < OPS:
            @pl.when(has_lower)
            def _():
                v_copy(op + 1, z, h).start()
        if op == 0:
            dot_into(0, image, image)
        elif op == 1:
            dot_into(1, r0[:, z, here], image)
            dot_into(2, image, image)

    pieces = [(d, h) for d in range(secs) for h in range(chunks)]

    loads[0].wait()
    pl.semaphore_wait(barrier, 1 + has_lower.astype(jnp.int32) + has_upper.astype(jnp.int32))

    @pl.when(has_lower)
    def _():
        for d, h in pieces:
            v_copy(0, d, h).start()

    loads[1].wait()
    send_edges(0)
    if far:
        reach_signal(0)
    loads[2].wait()
    loads[3].wait()
    for k in range(3):
        for z in range(secs):
            inside = jnp.where(g * secs + z + k + 1 < n * secs, 1.0, 0.0).astype(jnp.float32)
            for h in range(chunks):
                target = columns_at + dlt[k, z, rows_at(h)] - 4
                valid = (target >= 0) & (target < cols)
                wei[k, z, rows_at(h)] = jnp.where(valid, wei[k, z, rows_at(h)], 0.0) * inside
    loads[4].wait()
    for z in range(secs):
        for h in range(chunks):
            last = jnp.where((t == 1) & (row_at == HALF - 1), 0.0, 1.0) if h == chunks - 1 else 1.0
            vc[z, rows_at(h)] = (
                stiff[1, z] * jnp.where(spr[1, z, rows_at(h)] > 0, 1.0, 0.0).astype(jnp.float32) * last
            )
            right = stiff[0, z] * jnp.where(
                (spr[0, z, rows_at(h)] > 0) & (columns_at < cols - 1), 1.0, 0.0
            ).astype(jnp.float32)
            hc[z, rows_at(h)] = right
            left = rolled(right, 1)
            hl[z, rows_at(h)] = left
            diag[z, rows_at(h)] = dam[z, rows_at(h)] + right + left
    e_copy(0).wait_recv()
    for z in range(secs):
        k = 2 * secs + z
        edge = jnp.where(t == 1, stiff[1, z] * erecv[0, k : k + 1, :], 0.0)
        for h in range(chunks):
            if h == 0:
                above = jnp.where(row_at == 0, edge, pltpu.roll(vc[z, rows_at(h)], 1, 0))
            else:
                above = vc[z, pl.ds(h * HALF - 1, HALF)]
            va[z, rows_at(h)] = above
            diag[z, rows_at(h)] = diag[z, rows_at(h)] + vc[z, rows_at(h)] + above
    loads[5].wait()

    def reduce_start():
        packed = jnp.zeros((8, LANES), jnp.float32)
        sub = lax.broadcasted_iota(jnp.int32, (8, LANES), 0)
        for i in range(4):
            row = jnp.sum(dots[i], axis=0, keepdims=True)
            part = row[:, 0:LANES]
            for c in range(LANES, cols, LANES):
                part = part + row[:, c : c + LANES]
            packed = jnp.where(sub == i, part, packed)
        esend[OPS, 0:8, 0:LANES] = packed
        e_copy(OPS).start()
        e_copy(OPS).wait_recv()
        sall[...] = packed + erecv[OPS, 0:8, 0:LANES]
        pushes = []
        for j in range(1, n):
            pushes.append(
                pltpu.make_async_remote_copy(
                    sall, gath.at[j - 1], gs_sem.at[j - 1], gr_sem.at[j - 1],
                    device_id={"gz": lax.rem(g + j, n), "ta": t}, device_id_type=MESH,
                )
            )
        for push in pushes:
            push.start()
        return pushes

    for op in range(OPS):
        for h in range(chunks):
            own(op, h)
        if op > 0:
            e_copy(op).wait_recv()
        vertical(op)
        reach_step()
        for d, h in pieces:
            cross(op, d, h)
        if op == OPS - 1:
            while pending:
                reach_step()
            pushes = reduce_start()
        else:
            reach_step()
        for z, h in pieces:
            finish(op, z, h)
        if op + 1 < OPS:
            send_edges(op + 1)

    for push in pushes:
        push.wait_recv()
    total = sall[...]
    for j in range(1, n):
        total = total + gath[j - 1]
    total = jnp.sum(total, axis=1, keepdims=True)
    rr, rm, mm, mq = (total[i : i + 1, :] for i in range(4))
    alpha0 = rr / rm
    rr1 = alpha0 * (alpha0 * mm) - rr
    ratio = rr1 / rr
    one = 1.0 + ratio
    curve = one * one * rm - 2.0 * one * alpha0 * mm + alpha0 * alpha0 * mq
    alpha1 = rr1 / curve
    c1 = alpha0 + alpha1 * one
    c2 = alpha0 * alpha1
    for z in range(secs):
        for h in range(chunks):
            here = rows_at(h)
            for comp in range(2):
                a = r0[comp, z, here]
                b = m0[comp, z, here]
                upd[comp, z, here] = c1 * a - c2 * b
                res[comp, z, here] = a - c1 * b + c2 * qbuf[comp, z, here]

    for push in pushes:
        push.wait_send()
    for op in range(OPS + 1):
        e_copy(op).wait_send()

    @pl.when(has_lower)
    def _():
        for op in range(OPS):
            for d, h in pieces:
                v_copy(op, d, h).wait_send()

    @pl.when(has_upper)
    def _():
        for op in range(OPS):
            for d, h in pieces:
                t_copy(op, d, h).wait_send()


def body(position, gaps, weights, deltas, springs, damping, stiffness):
    secs, rows, cols = damping.shape
    n = lax.axis_size("gz")
    chunks = rows // HALF
    f32, i32 = jnp.float32, jnp.int32
    edge = -(-3 * secs // 8) * 8
    dma = pltpu.SemaphoreType.DMA
    out = pltpu.VMEM(position.shape, f32)
    anyspace = pl.BlockSpec(memory_space=pl.ANY)
    vmem = pl.BlockSpec(memory_space=pltpu.VMEM)
    field = pltpu.VMEM(position.shape, f32)
    plane = pltpu.VMEM(damping.shape, f32)
    exchange = pltpu.VMEM((OPS,) + position.shape, f32)
    piece_sems = dma((OPS, secs * chunks))
    return pl.pallas_call(
        functools.partial(kernel, n),
        out_shape=(out, out),
        in_specs=[anyspace] * 6 + [pl.BlockSpec(memory_space=pltpu.SMEM)],
        out_specs=(vmem, vmem),
        scratch_shapes=[
            field, field, field,
            exchange, exchange, exchange,
            pltpu.VMEM((OPS + 1, edge, cols), f32),
            pltpu.VMEM((OPS + 1, edge, cols), f32),
            pltpu.VMEM((8, LANES), f32),
            pltpu.VMEM((n - 1, 8, LANES), f32),
            pltpu.VMEM(gaps.shape, f32),
            pltpu.VMEM(weights.shape, f32),
            pltpu.VMEM(deltas.shape, i32),
            pltpu.VMEM(springs.shape, i32),
            plane, plane, plane, plane, plane, plane,
            field, field,
            pltpu.VMEM((4, HALF, cols), f32),
            dma((6,)),
            piece_sems, piece_sems, piece_sems, piece_sems,
            dma((OPS + 1,)), dma((OPS + 1,)),
            dma((n - 1,)), dma((n - 1,)),
            pltpu.SemaphoreType.REGULAR((max(len(doublings(n)), 1),)),
        ],
        compiler_params=pltpu.CompilerParams(
            collective_id=0, has_side_effects=True, vmem_limit_bytes=VMEM - 2 * 4 * position.size
        ),
    )(*[pltpu.with_memory_space_constraint(x, pltpu.HBM) for x in (position, gaps, weights, deltas, springs, damping)], stiffness)


def solution(mesh):
    return jax.shard_map(
        body,
        mesh=mesh,
        in_specs=(
            P(None, "gz", "ta", None),
            P(None, None, "gz", "ta", None),
            P(None, "gz", "ta", None),
            P(None, "gz", "ta", None),
            P(None, "gz", "ta", None),
            P("gz", "ta", None),
            P(None, "gz"),
        ),
        out_specs=(P(None, "gz", "ta", None), P(None, "gz", "ta", None)),
        check_vma=False,
    )
```

time: 48.1 us -> 41.7 us (0.87)
  Pallas kernels: 44.9 us -> 39.5 us
  local copies, waits for them, and re-layouts: 2.34 us -> 1.36 us
    pallas_call x1, Pallas kernels: 44.9 us -> 39.5 us  [body(): pl.pallas_call(functools.partial(kernel, n), out_shape=(out, out), in_spe...]
    unnamed x4 -> x2, local copies, waits for them, and re-layouts: 2.34 us -> 1.36 us
where the time goes in v1:
time: 41.7 us; the launch traced here: 41.5 us
  Pallas kernels  39.5 us (95%)
  local copies, waits for them, and re-layouts  1.36 us (3%)
  between operations  0.64 us (2%)
    pallas_call x1, Pallas kernels, body(): pl.pallas_call(functools.partial(kernel, n), out_shape=(out, out), in_spe...  39.5 us
    unnamed x2, local copies, waits for them, and re-layouts  1.36 us

profile of v1, /device:TPU:0, one launch (start us, length us, event | category | flops | bytes accessed | tf_op | source)
XLA Modules:
  0.0 41.5 jit_solution(13283040538829635327)
XLA Ops:
  0.6 39.5 %shard_map.86 = (f32[2,3,16,512]{3,2,1,0:T(8,128)S(1)}, f32[2,3,16,512]{3,2,1,0:T(8,128)S(1)}) custom-call(f32[2,3,16,512]{3,2,1,0:T(8,128)} %pos_h.1, f32[2,3,3,16,512]{4,3,2,1,0:T(8,128)} %gaps_h.1, f32[3,3,16,512]{3,2,1,0:T(8,128)} %wei_h.1, s32[3,3,16,512]{3,2,1,0:T(8,128)} %del_h.1, s32[2,3,16,512]{3,2,1,0:T(8,128)} %spr_h.1, f32[3,16,512]{2,1,0:T(8,128)} %dam_h.1, ...), custom_call_target="tpu_custom_call" | custom-call | tf_op jit(solution)/shard_map/pallas_call | solution.py:413
  40.2 0.7 %copy.11 = f32[2,3,16,512]{3,2,1,0:T(8,128)} copy(f32[2,3,16,512]{3,2,1,0:T(8,128)S(1)} %get-tuple-element.2) | data formatting | bytes 393216
  40.8 0.7 %copy.12 = f32[2,3,16,512]{3,2,1,0:T(8,128)} copy(f32[2,3,16,512]{3,2,1,0:T(8,128)S(1)} %get-tuple-element.3) | data formatting | bytes 393216

commit v2 on v1

--- a/solution.py
+++ b/solution.py
@@ -29,10 +29,10 @@
 
 
 def kernel(
-    n, pos_h, gaps_h, wei_h, del_h, spr_h, dam_h, stiff,
-    upd, res,
-    pos, r0, m0, up, tsend, trecv, esend, erecv, sall, gath,
-    gaps, wei, dlt, spr, dam, vc, va, hc, hl, diag, accb, qbuf, dots,
+    n, pos_h, gaps_h, wei_h, del_h, spr_h, dam_h, stiff_h,
+    r0, m0, qbuf, coef,
+    stiff, pos, up, tsend, trecv, esend, erecv, sall, gath,
+    gaps, wei, dlt, spr, dam, vc, va, hc, hl, diag, accb, dots,
     load_sem, vs_sem, vr_sem, ts_sem, tr_sem, es_sem, er_sem, gs_sem, gr_sem, reach_sem,
 ):
     g = lax.axis_index("gz")
@@ -53,6 +53,7 @@
         pltpu.make_async_copy(wei_h, wei, load_sem.at[3]),
         pltpu.make_async_copy(dam_h, dam, load_sem.at[4]),
         pltpu.make_async_copy(gaps_h, gaps, load_sem.at[5]),
+        pltpu.make_async_copy(stiff_h, stiff, load_sem.at[6]),
     ]
     for load in loads:
         load.start()
@@ -85,18 +86,18 @@
     def v_copy(op, d, h):
         return pltpu.make_async_remote_copy(
             fields[op].at[:, d, rows_at(h)], up.at[op, :, d, rows_at(h)],
-            vs_sem.at[op, d * chunks + h], vr_sem.at[op, d * chunks + h], device_id=lower, device_id_type=MESH,
+            vs_sem.at[0], vr_sem.at[d * chunks + h], device_id=lower, device_id_type=MESH,
         )
 
     def t_copy(op, d, h):
         return pltpu.make_async_remote_copy(
             tsend.at[op, :, d, rows_at(h)], trecv.at[op, :, d, rows_at(h)],
-            ts_sem.at[op, d * chunks + h], tr_sem.at[op, d * chunks + h], device_id=upper, device_id_type=MESH,
+            ts_sem.at[0], tr_sem.at[d * chunks + h], device_id=upper, device_id_type=MESH,
         )
 
     def e_copy(op):
         return pltpu.make_async_remote_copy(
-            esend.at[op], erecv.at[op], es_sem.at[op], er_sem.at[op],
+            esend.at[op], erecv.at[op], es_sem.at[0], er_sem.at[op],
             device_id=other, device_id_type=MESH,
         )
 
@@ -165,58 +166,53 @@
             miss = fields[op][:, z, rows_at(h)] - got[i]
             if op == 0:
                 miss = miss - gaps[:, k, z, rows_at(h)]
-            out.append((z, k, miss, wei[k, z, rows_at(h)][None] * miss))
+            out.append((z, k, got[i], miss, wei[k, z, rows_at(h)][None] * miss))
         return out
 
     def scatter(terms, h):
         total = None
         for place in range(PLACES):
             part = None
-            for z, k, _, pulled in terms:
+            for z, k, _, _, pulled in terms:
                 one = jnp.where((dlt[k, z, rows_at(h)] == place)[None], pulled, 0.0)
                 part = one if part is None else part + one
             part = rolled(part, place - 4)
             total = part if total is None else total + part
         return total
 
-    def own(op, h):
+    def own_pairs(op, s, h):
         here = rows_at(h)
-        acc = []
+        terms = pulls(op, s, h)
+        for z, _, _, _, pulled in terms:
+            accb[:, z, here] = accb[:, z, here] + pulled
+        accb[:, s, here] = accb[:, s, here] - scatter(terms, h)
+
+    def own_springs(op, h):
+        here = rows_at(h)
         for z in range(secs):
-            center = fields[op][:, z, here]
-            acc.append(
-                diag[z, here][None] * center
-                - hc[z, here][None] * rolled(center, -1)
-                - hl[z, here][None] * rolled(center, 1)
-            )
-        for s in range(1, secs):
-            terms = pulls(op, s, h)
-            for z, _, _, pulled in terms:
-                acc[z] = acc[z] + pulled
-            acc[s] = acc[s] - scatter(terms, h)
-        for z in range(secs):
-            accb[:, z, here] = acc[z]
-
-    def vertical(op):
-        for h in range(chunks):
-            here = rows_at(h)
-            for z in range(secs):
-                for comp in range(2):
-                    k = comp * secs + z
-                    center = fields[op][comp, z, here]
-                    if h == 0:
-                        above = jnp.where(row_at == 0, erecv[op, k : k + 1, :], pltpu.roll(center, 1, 0))
-                    else:
-                        above = fields[op][comp, z, pl.ds(h * HALF - 1, HALF)]
-                    if h == chunks - 1:
-                        below = jnp.where(
-                            row_at == HALF - 1, erecv[op, k : k + 1, :], pltpu.roll(center, HALF - 1, 0)
-                        )
-                    else:
-                        below = fields[op][comp, z, pl.ds(h * HALF + 1, HALF)]
-                    accb[comp, z, here] = accb[comp, z, here] - vc[z, here] * below - va[z, here] * above
-                if op == OPS - 1:
-                    dot_into(3, fields[op][:, z, here], accb[:, z, here])
+            for comp in range(2):
+                k = comp * secs + z
+                center = fields[op][comp, z, here]
+                if h == 0:
+                    above = jnp.where(row_at == 0, erecv[op, k : k + 1, :], pltpu.roll(center, 1, 0))
+                else:
+                    above = fields[op][comp, z, pl.ds(h * HALF - 1, HALF)]
+                if h == chunks - 1:
+                    below = jnp.where(
+                        row_at == HALF - 1, erecv[op, k : k + 1, :], pltpu.roll(center, HALF - 1, 0)
+                    )
+                else:
+                    below = fields[op][comp, z, pl.ds(h * HALF + 1, HALF)]
+                accb[comp, z, here] = (
+                    accb[comp, z, here]
+                    + diag[z, here] * center
+                    - hc[z, here] * rolled(center, -1)
+                    - hl[z, here] * rolled(center, 1)
+                    - vc[z, here] * below
+                    - va[z, here] * above
+                )
+            if op == OPS - 1:
+                dot_into(3, fields[op][:, z, here], accb[:, z, here])
 
     def cross(op, d, h):
         @pl.when(has_upper)
@@ -230,10 +226,12 @@
         def _():
             t_copy(op, d, h).start()
 
-        for z, _, miss, pulled in terms:
-            accb[:, z, rows_at(h)] = accb[:, z, rows_at(h)] + pulled
+        started = d == 0
+        for z, _, partner, _, pulled in terms:
+            before = 0.0 if started else accb[:, z, rows_at(h)]
+            accb[:, z, rows_at(h)] = before + pulled
             if op == OPS - 1:
-                dot_into(3, miss, pulled)
+                dot_into(3, -partner, pulled)
 
     def finish(op, z, h):
         here = rows_at(h)
@@ -283,6 +281,7 @@
                 valid = (target >= 0) & (target < cols)
                 wei[k, z, rows_at(h)] = jnp.where(valid, wei[k, z, rows_at(h)], 0.0) * inside
     loads[4].wait()
+    loads[6].wait()
     for z in range(secs):
         for h in range(chunks):
             last = jnp.where((t == 1) & (row_at == HALF - 1), 0.0, 1.0) if h == chunks - 1 else 1.0
@@ -310,43 +309,43 @@
     loads[5].wait()
 
     def reduce_start():
-        packed = jnp.zeros((8, LANES), jnp.float32)
-        sub = lax.broadcasted_iota(jnp.int32, (8, LANES), 0)
+        quarter = LANES // 4
+        group = lax.broadcasted_iota(jnp.int32, (1, LANES), 1) // quarter
+        packed = jnp.zeros((1, LANES), jnp.float32)
         for i in range(4):
             row = jnp.sum(dots[i], axis=0, keepdims=True)
             part = row[:, 0:LANES]
             for c in range(LANES, cols, LANES):
                 part = part + row[:, c : c + LANES]
-            packed = jnp.where(sub == i, part, packed)
-        esend[OPS, 0:8, 0:LANES] = packed
-        e_copy(OPS).start()
-        e_copy(OPS).wait_recv()
-        sall[...] = packed + erecv[OPS, 0:8, 0:LANES]
-        pushes = []
-        for j in range(1, n):
-            pushes.append(
-                pltpu.make_async_remote_copy(
-                    sall, gath.at[j - 1], gs_sem.at[j - 1], gr_sem.at[j - 1],
-                    device_id={"gz": lax.rem(g + j, n), "ta": t}, device_id_type=MESH,
-                )
-            )
-        for push in pushes:
-            push.start()
-        return pushes
-
+            part = part + pltpu.roll(part, LANES // 2, 1)
+            part = part + pltpu.roll(part, quarter, 1)
+            packed = jnp.where(group == i, part, packed)
+        sall[...] = packed
+        for j in range(1, 2 * n):
+            pltpu.make_async_remote_copy(
+                sall, gath.at[j - 1], gs_sem.at[0], gr_sem.at[0],
+                device_id={"gz": lax.rem(g + j // 2, n), "ta": t if j % 2 == 0 else 1 - t},
+                device_id_type=MESH,
+            ).start()
+
+    everyone = pltpu.make_async_remote_copy(
+        gath, gath, gs_sem.at[0], gr_sem.at[0], device_id=other, device_id_type=MESH
+    )
     for op in range(OPS):
-        for h in range(chunks):
-            own(op, h)
-        if op > 0:
-            e_copy(op).wait_recv()
-        vertical(op)
         reach_step()
-        for d, h in pieces:
+        tasks = [functools.partial(own_pairs, op, s, h) for s in range(1, secs) for h in range(chunks)]
+        tasks += [functools.partial(own_springs, op, h) for h in range(chunks)]
+        share = -(-len(tasks) // len(pieces))
+        for i, (d, h) in enumerate(pieces):
             cross(op, d, h)
+            for task in tasks[i * share : (i + 1) * share]:
+                if task.func is own_springs and op > 0 and task.args[1] == 0:
+                    e_copy(op).wait_recv()
+                task()
         if op == OPS - 1:
             while pending:
                 reach_step()
-            pushes = reduce_start()
+            reduce_start()
         else:
             reach_step()
         for z, h in pieces:
@@ -354,13 +353,14 @@
         if op + 1 < OPS:
             send_edges(op + 1)
 
-    for push in pushes:
-        push.wait_recv()
+    everyone.wait_recv()
     total = sall[...]
-    for j in range(1, n):
-        total = total + gath[j - 1]
-    total = jnp.sum(total, axis=1, keepdims=True)
-    rr, rm, mm, mq = (total[i : i + 1, :] for i in range(4))
+    for i in range(2 * n - 1):
+        total = total + gath[i]
+    group = lax.broadcasted_iota(jnp.int32, (1, LANES), 1) // (LANES // 4)
+    rr, rm, mm, mq = (
+        jnp.sum(jnp.where(group == i, total, 0.0), axis=1, keepdims=True) for i in range(4)
+    )
     alpha0 = rr / rm
     rr1 = alpha0 * (alpha0 * mm) - rr
     ratio = rr1 / rr
@@ -369,31 +369,25 @@
     alpha1 = rr1 / curve
     c1 = alpha0 + alpha1 * one
     c2 = alpha0 * alpha1
-    for z in range(secs):
-        for h in range(chunks):
-            here = rows_at(h)
-            for comp in range(2):
-                a = r0[comp, z, here]
-                b = m0[comp, z, here]
-                upd[comp, z, here] = c1 * a - c2 * b
-                res[comp, z, here] = a - c1 * b + c2 * qbuf[comp, z, here]
-
-    for push in pushes:
-        push.wait_send()
-    for op in range(OPS + 1):
-        e_copy(op).wait_send()
+    coef[0:1, :] = jnp.broadcast_to(c1, (1, cols))
+    coef[1:2, :] = jnp.broadcast_to(c2, (1, cols))
+
+    everyone.wait_send()
+    pltpu.make_async_remote_copy(
+        esend, erecv, es_sem.at[0], er_sem.at[0], device_id=other, device_id_type=MESH
+    ).wait_send()
 
     @pl.when(has_lower)
     def _():
-        for op in range(OPS):
-            for d, h in pieces:
-                v_copy(op, d, h).wait_send()
+        pltpu.make_async_remote_copy(
+            up, up, vs_sem.at[0], vr_sem.at[0], device_id=lower, device_id_type=MESH
+        ).wait_send()
 
     @pl.when(has_upper)
     def _():
-        for op in range(OPS):
-            for d, h in pieces:
-                t_copy(op, d, h).wait_send()
+        pltpu.make_async_remote_copy(
+            tsend, trecv, ts_sem.at[0], tr_sem.at[0], device_id=upper, device_id_type=MESH
+        ).wait_send()
 
 
 def body(position, gaps, weights, deltas, springs, damping, stiffness):
@@ -409,36 +403,38 @@
     field = pltpu.VMEM(position.shape, f32)
     plane = pltpu.VMEM(damping.shape, f32)
     exchange = pltpu.VMEM((OPS,) + position.shape, f32)
-    piece_sems = dma((OPS, secs * chunks))
-    return pl.pallas_call(
+    r0, m0, q, coef = pl.pallas_call(
         functools.partial(kernel, n),
-        out_shape=(out, out),
-        in_specs=[anyspace] * 6 + [pl.BlockSpec(memory_space=pltpu.SMEM)],
-        out_specs=(vmem, vmem),
+        out_shape=(out, out, out, pltpu.VMEM((2, cols), f32)),
+        in_specs=[anyspace] * 7,
+        out_specs=(vmem,) * 4,
         scratch_shapes=[
-            field, field, field,
+            pltpu.SMEM(stiffness.shape, f32),
+            field,
             exchange, exchange, exchange,
-            pltpu.VMEM((OPS + 1, edge, cols), f32),
-            pltpu.VMEM((OPS + 1, edge, cols), f32),
-            pltpu.VMEM((8, LANES), f32),
-            pltpu.VMEM((n - 1, 8, LANES), f32),
+            pltpu.VMEM((OPS, edge, cols), f32),
+            pltpu.VMEM((OPS, edge, cols), f32),
+            pltpu.VMEM((1, LANES), f32),
+            pltpu.VMEM((2 * n - 1, 1, LANES), f32),
             pltpu.VMEM(gaps.shape, f32),
             pltpu.VMEM(weights.shape, f32),
             pltpu.VMEM(deltas.shape, i32),
             pltpu.VMEM(springs.shape, i32),
             plane, plane, plane, plane, plane, plane,
-            field, field,
+            field,
             pltpu.VMEM((4, HALF, cols), f32),
-            dma((6,)),
-            piece_sems, piece_sems, piece_sems, piece_sems,
-            dma((OPS + 1,)), dma((OPS + 1,)),
-            dma((n - 1,)), dma((n - 1,)),
+            dma((7,)),
+            dma((1,)), dma((secs * chunks,)), dma((1,)), dma((secs * chunks,)),
+            dma((1,)), dma((OPS,)),
+            dma((1,)), dma((1,)),
             pltpu.SemaphoreType.REGULAR((max(len(doublings(n)), 1),)),
         ],
         compiler_params=pltpu.CompilerParams(
-            collective_id=0, has_side_effects=True, vmem_limit_bytes=VMEM - 2 * 4 * position.size
+            collective_id=0, has_side_effects=True, vmem_limit_bytes=VMEM - 3 * 4 * position.size - 2 * 4 * LANES * HALF
         ),
-    )(*[pltpu.with_memory_space_constraint(x, pltpu.HBM) for x in (position, gaps, weights, deltas, springs, damping)], stiffness)
+    )(*[pltpu.with_memory_space_constraint(x, pltpu.HBM) for x in (position, gaps, weights, deltas, springs, damping, stiffness)])
+    c1, c2 = coef[0], coef[1]
+    return c1 * r0 - c2 * m0, r0 - c1 * m0 + c2 * q
 
 
 def solution(mesh):

time: 41.7 us -> 38 us (0.911)
  Pallas kernels: 39.5 us -> 36.4 us
  local copies, waits for them, and re-layouts: 1.36 us -> 0.01 us
  other arithmetic: 0 us -> 0.81 us
    pallas_call x1, Pallas kernels: 39.5 us -> 36.4 us  [body(): pl.pallas_call(functools.partial(kernel, n), out_shape=(out, out, out, pl...]
    unnamed x2 -> x0, local copies, waits for them, and re-layouts: 1.36 us -> none
    add x0 -> x1, other arithmetic: none -> 0.81 us  [body(): return (c1 * r0 - c2 * m0, r0 - c1 * m0 + c2 * q)]
where the time goes in v2:
time: 38 us; the launch traced here: 37.9 us
  Pallas kernels  36.4 us (96%)
  other arithmetic  0.81 us (2%)
  between operations  0.65 us (2%)
    pallas_call x1, Pallas kernels, body(): pl.pallas_call(functools.partial(kernel, n), out_shape=(out, out, out, pl...  36.4 us
    add x1, other arithmetic, body(): return (c1 * r0 - c2 * m0, r0 - c1 * m0 + c2 * q)  0.81 us

profile of v2, /device:TPU:0, one launch (start us, length us, event | category | flops | bytes accessed | tf_op | source)
XLA Modules:
  0.0 37.9 jit_solution(9913310266927034766)
XLA Ops:
  0.6 36.4 %shard_map.86 = (f32[2,3,16,512]{3,2,1,0:T(8,128)S(1)}, f32[2,3,16,512]{3,2,1,0:T(8,128)S(1)}, f32[2,3,16,512]{3,2,1,0:T(8,128)S(1)}, f32[2,512]{1,0:T(2,128)S(1)}) custom-call(f32[2,3,16,512]{3,2,1,0:T(8,128)} %pos_h.1, f32[2,3,3,16,512]{4,3,2,1,0:T(8,128)} %gaps_h.1, f32[3,3,16,512]{3,2,1,0:T(8,128)} %wei_h.1, s32[3,3,16,512]{3,2,1,0:T(8,128)} %del_h.1, ...), custom_call_target="tpu_custom_call" | custom-call | tf_op jit(solution)/shard_map/pallas_call | solution.py:406
  37.1 0.8 %multiply_add_fusion = (f32[2,3,16,512]{3,2,1,0:T(8,128)}, f32[2,3,16,512]{3,2,1,0:T(8,128)}) fusion(f32[2,3,16,512]{3,2,1,0:T(8,128)S(1)} %get-tuple-element.9, f32[2,3,16,512]{3,2,1,0:T(8,128)S(1)} %get-tuple-element.7, f32[2,3,16,512]{3,2,1,0:T(8,128)S(1)} %get-tuple-element.8, f32[512]{0:T(512)S(1)} %bitcast.3, f32[512]{0:T(512)S(1)} %bitcast.2), kind=kLoop, calls=%fused_computation | loop fusion | flops 344064 | bytes 987136 | tf_op jit(solution)/shard_map/add | solution.py:437
  (1 shorter events, 0.0 us)

commit v3 on v2

--- a/solution.py
+++ b/solution.py
@@ -222,9 +222,10 @@
         terms = pulls(op, secs + d, h)
         tsend[op, :, d, rows_at(h)] = scatter(terms, h)
 
-        @pl.when(has_upper)
-        def _():
-            t_copy(op, d, h).start()
+        if op < OPS - 1:
+            @pl.when(has_upper)
+            def _():
+                t_copy(op, d, h).start()
 
         started = d == 0
         for z, _, partner, _, pulled in terms:
@@ -258,6 +259,8 @@
             dot_into(2, image, image)
 
     pieces = [(d, h) for d in range(secs) for h in range(chunks)]
+
+    held = pieces
 
     loads[0].wait()
     pl.semaphore_wait(barrier, 1 + has_lower.astype(jnp.int32) + has_upper.astype(jnp.int32))
@@ -308,19 +311,26 @@
             diag[z, rows_at(h)] = diag[z, rows_at(h)] + vc[z, rows_at(h)] + above
     loads[5].wait()
 
+    quarter = LANES // 4
+    group = lax.broadcasted_iota(jnp.int32, (1, LANES), 1) // quarter
+
+    def folded(i):
+        row = jnp.sum(dots[i], axis=0, keepdims=True)
+        part = row[:, 0:LANES]
+        for c in range(LANES, cols, LANES):
+            part = part + row[:, c : c + LANES]
+        part = part + pltpu.roll(part, LANES // 2, 1)
+        return part + pltpu.roll(part, quarter, 1)
+
+    def pack_known():
+        packed = jnp.zeros((1, LANES), jnp.float32)
+        for i in range(OPS):
+            packed = jnp.where(group == i, folded(i), packed)
+        sall[...] = packed
+
     def reduce_start():
-        quarter = LANES // 4
-        group = lax.broadcasted_iota(jnp.int32, (1, LANES), 1) // quarter
-        packed = jnp.zeros((1, LANES), jnp.float32)
-        for i in range(4):
-            row = jnp.sum(dots[i], axis=0, keepdims=True)
-            part = row[:, 0:LANES]
-            for c in range(LANES, cols, LANES):
-                part = part + row[:, c : c + LANES]
-            part = part + pltpu.roll(part, LANES // 2, 1)
-            part = part + pltpu.roll(part, quarter, 1)
-            packed = jnp.where(group == i, part, packed)
-        sall[...] = packed
+        part = folded(OPS)
+        sall[...] = jnp.where(group == OPS, part, sall[...])
         for j in range(1, 2 * n):
             pltpu.make_async_remote_copy(
                 sall, gath.at[j - 1], gs_sem.at[0], gr_sem.at[0],
@@ -346,18 +356,24 @@
             while pending:
                 reach_step()
             reduce_start()
+
+            @pl.when(has_upper)
+            def _():
+                for d, h in held:
+                    t_copy(op, d, h).start()
         else:
             reach_step()
         for z, h in pieces:
             finish(op, z, h)
         if op + 1 < OPS:
             send_edges(op + 1)
+        if op == OPS - 2:
+            pack_known()
 
     everyone.wait_recv()
     total = sall[...]
     for i in range(2 * n - 1):
         total = total + gath[i]
-    group = lax.broadcasted_iota(jnp.int32, (1, LANES), 1) // (LANES // 4)
     rr, rm, mm, mq = (
         jnp.sum(jnp.where(group == i, total, 0.0), axis=1, keepdims=True) for i in range(4)
     )

time: 38 us -> 37.2 us (0.979)
  Pallas kernels: 36.4 us -> 35.6 us
    pallas_call x1, Pallas kernels: 36.4 us -> 35.6 us  [body(): pl.pallas_call(functools.partial(kernel, n), out_shape=(out, out, out, pl...]
where the time goes in v3:
time: 37.2 us; the launch traced here: 37 us
  Pallas kernels  35.6 us (96%)
  other arithmetic  0.81 us (2%)
  between operations  0.65 us (2%)
    pallas_call x1, Pallas kernels, body(): pl.pallas_call(functools.partial(kernel, n), out_shape=(out, out, out, pl...  35.6 us
    add x1, other arithmetic, body(): return (c1 * r0 - c2 * m0, r0 - c1 * m0 + c2 * q)  0.81 us

profile of v3, /device:TPU:0, one launch (start us, length us, event | category | flops | bytes accessed | tf_op | source)
XLA Modules:
  0.0 37.0 jit_solution(13640915640586036049)
XLA Ops:
  0.6 35.6 %shard_map.86 = (f32[2,3,16,512]{3,2,1,0:T(8,128)S(1)}, f32[2,3,16,512]{3,2,1,0:T(8,128)S(1)}, f32[2,3,16,512]{3,2,1,0:T(8,128)S(1)}, f32[2,512]{1,0:T(2,128)S(1)}) custom-call(f32[2,3,16,512]{3,2,1,0:T(8,128)} %pos_h.1, f32[2,3,3,16,512]{4,3,2,1,0:T(8,128)} %gaps_h.1, f32[3,3,16,512]{3,2,1,0:T(8,128)} %wei_h.1, s32[3,3,16,512]{3,2,1,0:T(8,128)} %del_h.1, ...), custom_call_target="tpu_custom_call" | custom-call | tf_op jit(solution)/shard_map/pallas_call | solution.py:422
  36.2 0.8 %multiply_add_fusion = (f32[2,3,16,512]{3,2,1,0:T(8,128)}, f32[2,3,16,512]{3,2,1,0:T(8,128)}) fusion(f32[2,3,16,512]{3,2,1,0:T(8,128)S(1)} %get-tuple-element.9, f32[2,3,16,512]{3,2,1,0:T(8,128)S(1)} %get-tuple-element.7, f32[2,3,16,512]{3,2,1,0:T(8,128)S(1)} %get-tuple-element.8, f32[512]{0:T(512)S(1)} %bitcast.3, f32[512]{0:T(512)S(1)} %bitcast.2), kind=kLoop, calls=%fused_computation | loop fusion | flops 344064 | bytes 987136 | tf_op jit(solution)/shard_map/add | solution.py:453
  (1 shorter events, 0.0 us)
